TPU v7x, 8 devices: a whole 2x2x1 slice. The times are simulated.
8 devices in a mesh: dp: 1 (over z), ctx: 8 (over y, x, core).
Axes of the slice: x: 2, y: 2, z: 1, core: 2. Of those that a mesh axis runs over, the one named last changes fastest.
Arguments:
- x_chunk: bfloat16 [2048, 2560], P(('dp', 'ctx'))
- cache_len: int32 [1], P('dp')
- k_cache: bfloat16 [2, 16384, 20, 128], P(None, ('dp', 'ctx'))
- v_cache: bfloat16 [2, 16384, 20, 128], P(None, ('dp', 'ctx'))
- k_local: bfloat16 [2, 256, 20, 128], P(None, 'dp')
- v_local: bfloat16 [2, 256, 20, 128], P(None, 'dp')
- g_attn: bfloat16 [4, 2560], replicated
- g_mlp: bfloat16 [4, 2560], replicated
- w_q: bfloat16 [4, 2560, 2560], replicated
- w_k: bfloat16 [4, 2560, 2560], replicated
- w_v: bfloat16 [4, 2560, 2560], replicated
- w_o: bfloat16 [4, 2560, 2560], replicated
- w_gate: bfloat16 [4, 2560, 10240], replicated
- w_up: bfloat16 [4, 2560, 10240], replicated
- w_down: bfloat16 [4, 10240, 2560], replicated
Outputs:
- output: bfloat16 [2048, 2560], P(('dp', 'ctx'))
All inputs are finite; a program needn't handle non-finite values.
Results may differ from a plain program's by a relative error of at most 0.02.
Values are sent between devices in bfloat16 or wider.
A program may use at most 3.5 GiB of HBM per device.

v0:
```python
import functools
import jax
import jax.numpy as jnp
from jax import lax
from jax.experimental import pallas as pl
from jax.experimental.pallas import tpu as pltpu
from jax.sharding import PartitionSpec as P

EPS = 1e-6
CH = 512
NS = 3
KT = 1024
HD = 128
LOG2E = 1.4426950408889634
SCALE2 = LOG2E * HD ** -0.5
NEG = -jnp.inf
BF = jnp.bfloat16
F32 = jnp.float32
VLIM = 60 * 2 ** 20

VM = pl.BlockSpec(memory_space=pltpu.VMEM)
HB = pl.BlockSpec(memory_space=pl.ANY)
SM = pl.BlockSpec(memory_space=pltpu.SMEM)


def norm_rows(xf, gain):
    inv = lax.rsqrt(jnp.mean(xf * xf, axis=-1, keepdims=True) + EPS)
    return (xf * inv * gain).astype(BF)


def col(c, w):
    return pl.ds(pl.multiple_of(c * w, w), w)


def layer_kernel(layer, nxt, rows, d, ff):
    has_tail = layer is not None
    na = d // CH if has_tail else 0
    nb = ff // CH if has_tail else 0
    nq = d // CH
    nc = 3 * nq if nxt is not None else 0
    total = na + nb + nc

    def body(*refs):
        refs = list(refs)
        if has_tail:
            o_ref = refs.pop(0)
        x_ref = refs.pop(0)
        if has_tail:
            gm_ref = refs.pop(0)
        if nc:
            ga_ref = refs.pop(0)
        if has_tail:
            wo, wg, wu, wd = [refs.pop(0) for _ in range(4)]
        if nc:
            wq, wk, wv = [refs.pop(0) for _ in range(3)]
        if has_tail:
            xo_ref = refs.pop(0)
        if nc:
            qkv_refs = [refs.pop(0) for _ in range(3)]
        ba, bb, bd, h_s, acc, sa, sb, sd = refs

        def cp(w, l, c, buf, sem, slot, by_rows=False):
            src = w.at[l, pl.ds(pl.multiple_of(c * CH, CH), CH), :] if by_rows else w.at[l, :, col(c, CH)]
            return pltpu.make_async_copy(src, buf.at[slot], sem.at[slot])

        def start(t):
            slot = lax.rem(t, NS)
            if has_tail:
                @pl.when(t < na)
                def _():
                    cp(wo, layer, t, bd, sd, slot, True).start()

                @pl.when((t >= na) & (t < na + nb))
                def _():
                    c = t - na
                    cp(wg, layer, c, ba, sa, slot).start()
                    cp(wu, layer, c, bb, sb, slot).start()
                    cp(wd, layer, c, bd, sd, slot, True).start()
            if nc:
                for i, w in enumerate((wq, wk, wv)):
                    lo = na + nb + i * nq

                    @pl.when((t >= lo) & (t < lo + nq))
                    def _():
                        cp(w, nxt, t - lo, ba, sa, slot).start()

        for t in range(NS - 1):
            start(jnp.int32(t))
        if has_tail:
            acc[...] = x_ref[...].astype(F32)

            def pa(t, _):
                start(t + NS - 1)
                slot = lax.rem(t, NS)
                cp(wo, layer, 0, bd, sd, slot, True).wait()
                acc[...] += jnp.dot(o_ref[:, col(t, CH)], bd[slot], preferred_element_type=F32)
                return 0
            lax.fori_loop(0, na, pa, 0)
            xm = acc[...].astype(BF).astype(F32)
            h_s[...] = norm_rows(xm, gm_ref[layer:layer + 1, :].astype(F32))
            acc[...] = xm

            def pb(t, _):
                @pl.when(t + NS - 1 < total)
                def _():
                    start(t + NS - 1)
                slot = lax.rem(t, NS)
                cp(wg, layer, 0, ba, sa, slot).wait()
                gate = jnp.dot(h_s[...], ba[slot], preferred_element_type=F32)
                cp(wu, layer, 0, bb, sb, slot).wait()
                up = jnp.dot(h_s[...], bb[slot], preferred_element_type=F32)
                act = (jax.nn.gelu(gate, approximate=True) * up).astype(BF)
                cp(wd, layer, 0, bd, sd, slot, True).wait()
                acc[...] += jnp.dot(act, bd[slot], preferred_element_type=F32)
                return 0
            lax.fori_loop(na, na + nb, pb, 0)
            xb = acc[...].astype(BF)
            xo_ref[...] = xb
        else:
            xb = x_ref[...]
        if nc:
            h_s[...] = norm_rows(xb.astype(F32), ga_ref[nxt:nxt + 1, :].astype(F32))
            for i, w in enumerate((wq, wk, wv)):
                lo = na + nb + i * nq

                def pc(t, _):
                    @pl.when(t + NS - 1 < total)
                    def _():
                        start(t + NS - 1)
                    slot = lax.rem(t, NS)
                    cp(w, nxt, 0, ba, sa, slot).wait()
                    qkv_refs[i][:, col(t - lo, CH)] = jnp.dot(h_s[...], ba[slot], preferred_element_type=F32).astype(BF)
                    return 0
                lax.fori_loop(lo, lo + nq, pc, 0)

    n_in_v = (3 if has_tail else 1) + (1 if nc else 0)
    n_in_h = (4 if has_tail else 0) + (3 if nc else 0)
    outs = []
    if has_tail:
        outs.append(jax.ShapeDtypeStruct((rows, d), BF))
    if nc:
        outs += [jax.ShapeDtypeStruct((rows, d), BF)] * 3
    flops = 2 * rows * d * ((d + 3 * ff if has_tail else 0) + (3 * d if nc else 0))
    return pl.pallas_call(
        body, out_shape=outs, in_specs=[VM] * n_in_v + [HB] * n_in_h, out_specs=[VM] * len(outs),
        scratch_shapes=[
            pltpu.VMEM((NS, d, CH), BF), pltpu.VMEM((NS, d, CH), BF), pltpu.VMEM((NS, CH, d), BF),
            pltpu.VMEM((rows, d), BF), pltpu.VMEM((rows, d), F32),
            pltpu.SemaphoreType.DMA((NS,)), pltpu.SemaphoreType.DMA((NS,)), pltpu.SemaphoreType.DMA((NS,))],
        compiler_params=pltpu.CompilerParams(vmem_limit_bytes=VLIM),
        cost_estimate=pl.CostEstimate(flops=flops, bytes_accessed=flops // rows, transcendentals=0),
        name=f"layer_{layer}_{nxt}")


def local_attention(pair, rows, d, n_chip):
    hg = d // HD // n_chip
    width = d // n_chip

    def body(dev_ref, q_ref, k_ref, v_ref, kh_ref, vh_ref, kl_ref, vl_ref, o_ref):
        first = dev_ref[0] == 0
        key_id = lax.broadcasted_iota(jnp.int32, (2 * rows, rows), 0)
        row_id = lax.broadcasted_iota(jnp.int32, (2 * rows, rows), 1)
        band = (key_id > row_id) & (key_id <= row_id + rows)

        def chip(g, _):
            for j in range(hg):
                c = pl.ds(pl.multiple_of(g * width + j * HD, HD), HD)
                k = jnp.concatenate([jnp.where(first, kl_ref[0, g * hg + j], kh_ref[:, c]), k_ref[:, c]], axis=0)
                v = jnp.concatenate([jnp.where(first, vl_ref[0, g * hg + j], vh_ref[:, c]), v_ref[:, c]], axis=0)
                s = lax.dot_general(k, q_ref[:, c], (((1,), (1,)), ((), ())), preferred_element_type=F32)
                s = jnp.where(band, s, NEG)
                m = jnp.max(s, axis=0, keepdims=True)
                p = jnp.exp2(s * SCALE2 - m * SCALE2)
                l = jnp.sum(p, axis=0, keepdims=True)
                o = lax.dot_general(v, p.astype(BF), (((0,), (0,)), ((), ())), preferred_element_type=F32)
                o_ref[:, c] = (o / l).T.astype(BF)
            return 0
        lax.fori_loop(0, n_chip, chip, 0)

    loc = pl.BlockSpec((1, d // HD, rows, HD), lambda i: (pair, 0, 0, 0))
    return pl.pallas_call(
        body, grid=(1,), out_shape=jax.ShapeDtypeStruct((rows, d), BF),
        in_specs=[SM] + [VM] * 5 + [loc, loc], out_specs=pl.BlockSpec((rows, d), lambda i: (0, 0)),
        compiler_params=pltpu.CompilerParams(vmem_limit_bytes=VLIM),
        cost_estimate=pl.CostEstimate(flops=8 * rows * rows * d, bytes_accessed=16 * rows * d, transcendentals=0),
        name=f"local_{pair}")


def global_attention(pair, slot_rows, rows, d, n_chip):
    n_dev = 2 * n_chip
    nq = n_dev * rows
    qh = nq // 2
    heads = d // HD
    hh = heads // 2
    half = hh * HD
    cache = 2 * slot_rows
    keys = cache + 2 * rows
    st = HD + 8
    n_tile = cache // KT
    low = -3e38

    def body(len_ref, q_ref, kn_ref, vn_ref, kc, vc, o_ref, kx, vx,
             qb, knp, vnp, ks, vs, m_s, l_s, acc, s_a, s_b, stage, part,
             q_snd, q_rcv, x_snd, x_rcv, n_snd, n_rcv, p_snd, p_rcv, sk, sv):
        dev = lax.axis_index('ctx')
        core = lax.rem(dev, 2)
        g_me = lax.div(dev, 2)
        mate = dev + 1 - 2 * core

        def remote(src, dst, snd, rcv, to):
            return pltpu.make_async_remote_copy(
                src_ref=src, dst_ref=dst, send_sem=snd, recv_sem=rcv,
                device_id={'ctx': to}, device_id_type=pl.DeviceIdType.MESH)

        def head_cols(b, i):
            return pl.ds(pl.multiple_of((b * hh + i) * HD, HD), HD)

        def dev_rows(t):
            return pl.ds(pl.multiple_of(t * rows, rows), rows)

        def q_copy(i, k):
            to = lax.rem(dev + k, n_dev)
            return remote(q_ref.at[:, head_cols(lax.rem(to, 2), i)], qb.at[i, dev_rows(dev), :],
                          q_snd.at[i, k - 1], q_rcv.at[i, dev], to)

        def q_wait(i, k):
            src = lax.rem(dev + k, n_dev)
            remote(q_ref.at[:, head_cols(0, i)], qb.at[i, dev_rows(src), :],
                   q_snd.at[i, k - 1], q_rcv.at[i, src], src).wait_recv()

        def x_copy(i, w):
            src, dst = ((kc, kx), (vc, vx))[w]
            return remote(src.at[pair, (1 - core) * hh + i], dst.at[i], x_snd.at[w, i], x_rcv.at[w, i], mate)

        def n_copy(w):
            src, dst = ((kn_ref, knp), (vn_ref, vnp))[w]
            return remote(src.at[:, pl.ds(pl.multiple_of((1 - core) * half, half), half)], dst,
                          n_snd.at[w], n_rcv.at[w], mate)

        def p_copy(i, k):
            to = lax.rem(dev + k, n_dev)
            return remote(stage.at[i, to], part.at[core * hh + i, g_me],
                          p_snd.at[i, k - 1], p_rcv.at[core * hh + i, g_me], to)

        def own(i, slot, w):
            src, dst, sem = ((kc, ks, sk), (vc, vs, sv))[w]
            return pltpu.make_async_copy(src.at[pair, core * hh + i], dst.at[slot, 0:slot_rows, :], sem.at[slot, 0])

        def mated(i, slot, w):
            src, dst, sem = ((kx, ks, sk), (vx, vs, sv))[w]
            return pltpu.make_async_copy(src.at[i], dst.at[slot, slot_rows:cache, :], sem.at[slot, 1])

        bar = pltpu.get_barrier_semaphore()
        for k in range(1, n_dev):
            pl.semaphore_signal(bar, inc=1, device_id={'ctx': lax.rem(dev + k, n_dev)}, device_id_type=pl.DeviceIdType.MESH)
        pl.semaphore_wait(bar, n_dev - 1)

        for w in range(2):
            own(0, 0, w).start()
            x_copy(0, w).start()
            n_copy(w).start()

        def send_q(i, _):
            for k in range(1, n_dev):
                q_copy(i, k).start()
            return 0
        lax.fori_loop(0, hh, send_q, 0)

        def send_x(i, _):
            for w in range(2):
                x_copy(i, w).start()
            return 0
        lax.fori_loop(1, hh, send_x, 0)
        for w in range(2):
            x_copy(0, w).wait_recv()
            mated(0, 0, w).start()
            n_copy(w).wait_recv()

        n = len_ref[0]

        def one_head(i, _):
            slot = lax.rem(i, 2)

            @pl.when(i + 1 < hh)
            def _():
                for w in range(2):
                    own(i + 1, 1 - slot, w).start()
                    x_copy(i + 1, w).wait_recv()
                    mated(i + 1, 1 - slot, w).start()
            mine = head_cols(core, i)
            there = head_cols(0, i)
            ks[slot, cache:cache + rows, :] = kn_ref[:, mine]
            ks[slot, cache + rows:keys, :] = knp[:, there]
            vs[slot, cache:cache + rows, :] = vn_ref[:, mine]
            vs[slot, cache + rows:keys, :] = vnp[:, there]
            qb[i, dev_rows(dev), :] = q_ref[:, mine]
            m_s[...] = jnp.full(m_s.shape, low, F32)
            l_s[...] = jnp.zeros(l_s.shape, F32)
            acc[...] = jnp.zeros(acc.shape, F32)
            for k in range(1, n_dev):
                q_wait(i, k)
            for w in range(2):
                own(i, slot, w).wait()
                mated(i, slot, w).wait()

            def scores(start, size, hf):
                k = ks[slot, pl.ds(start, size), :]
                q = qb[i, hf * qh:(hf + 1) * qh, :]
                return lax.dot_general(k, q, (((1,), (1,)), ((), ())), preferred_element_type=F32)

            def absorb(s, start, size, hf):
                v = vs[slot, pl.ds(start, size), :]
                c = slice(hf * qh, (hf + 1) * qh)
                m0 = m_s[:, c]
                m1 = jnp.maximum(m0, jnp.max(s, axis=0, keepdims=True))
                a = jnp.exp2((m0 - m1) * SCALE2)
                p = jnp.exp2(s * SCALE2 - m1 * SCALE2)
                l_s[:, c] = l_s[:, c] * a + jnp.sum(p, axis=0, keepdims=True)
                m_s[:, c] = m1
                acc[:, c] = acc[:, c] * a + lax.dot_general(v, p.astype(BF), (((0,), (0,)), ((), ())), preferred_element_type=F32)

            def tile(t):
                return pl.multiple_of(t * KT, KT)

            def valid(s, t):
                per = slot_rows // KT
                owner = jnp.where(t < per, dev, mate)
                left = n - owner * slot_rows - lax.rem(t, per) * KT
                return jnp.where(lax.broadcasted_iota(jnp.int32, s.shape, 0) < left, s, NEG)

            s_a[...] = scores(0, KT, 0)

            def tiles(t, _):
                s_b[...] = scores(tile(t), KT, 1)
                absorb(valid(s_a[...], t), tile(t), KT, 0)
                s_a[...] = scores(tile(t + 1), KT, 0)
                absorb(valid(s_b[...], t), tile(t), KT, 1)
                return 0
            lax.fori_loop(0, n_tile - 1, tiles, 0)
            last = n_tile - 1
            s_b[...] = scores(last * KT, KT, 1)
            absorb(valid(s_a[...], last), last * KT, KT, 0)
            absorb(valid(s_b[...], last), last * KT, KT, 1)
            for hf in range(2):
                s = scores(cache, 2 * rows, hf)
                r = lax.broadcasted_iota(jnp.int32, s.shape, 0)
                qi = lax.broadcasted_iota(jnp.int32, s.shape, 1) + hf * qh
                pos = jnp.where(r < rows, r + dev * rows, r - rows + mate * rows)
                absorb(jnp.where(pos <= qi, s, NEG), cache, 2 * rows, hf)
            for t in range(n_dev):
                c = slice(t * rows, (t + 1) * rows)
                stage[i, t, 0:HD, :] = acc[:, c]
                stage[i, t, HD:HD + 1, :] = m_s[:, c]
                stage[i, t, HD + 1:HD + 2, :] = l_s[:, c]
            part[core * hh + i, g_me] = stage[i, dev]
            for k in range(1, n_dev):
                p_copy(i, k).start()
            return 0
        lax.fori_loop(0, hh, one_head, 0)

        def finish(i, _):
            for b in range(2):
                h = b * hh + i
                for g in range(n_chip):
                    src = 2 * g + b

                    @pl.when(src != dev)
                    def _():
                        remote(stage.at[i, 0], part.at[h, g], p_snd.at[i, 0], p_rcv.at[h, g], mate).wait_recv()
                m = [part[h, g, HD:HD + 1, :] for g in range(n_chip)]
                top = functools.reduce(jnp.maximum, m)
                num = 0.0
                den = 0.0
                for g in range(n_chip):
                    a = jnp.exp2((m[g] - top) * SCALE2)
                    num = num + part[h, g, 0:HD, :] * a
                    den = den + part[h, g, HD + 1:HD + 2, :] * a
                o_ref[:, head_cols(b, i)] = (num / den).T.astype(BF)
            return 0
        lax.fori_loop(0, hh, finish, 0)

        def drain(i, _):
            for k in range(1, n_dev):
                q_copy(i, k).wait_send()
                p_copy(i, k).wait_send()
            for w in range(2):
                x_copy(i, w).wait_send()
            return 0
        lax.fori_loop(0, hh, drain, 0)
        for w in range(2):
            n_copy(w).wait_send()

    flops = 4 * nq * keys * half
    dma = pltpu.SemaphoreType.DMA
    xs = jax.ShapeDtypeStruct((hh, slot_rows, HD), BF)
    return pl.pallas_call(
        body, out_shape=[jax.ShapeDtypeStruct((rows, d), BF), xs, xs],
        in_specs=[SM, VM, VM, VM, HB, HB], out_specs=[VM, HB, HB],
        scratch_shapes=[
            pltpu.VMEM((hh, nq, HD), BF), pltpu.VMEM((rows, half), BF), pltpu.VMEM((rows, half), BF),
            pltpu.VMEM((2, keys, HD), BF), pltpu.VMEM((2, keys, HD), BF),
            pltpu.VMEM((1, nq), F32), pltpu.VMEM((1, nq), F32), pltpu.VMEM((HD, nq), F32),
            pltpu.VMEM((KT, qh), F32), pltpu.VMEM((KT, qh), F32),
            pltpu.VMEM((hh, n_dev, st, rows), F32), pltpu.VMEM((heads, n_chip, st, rows), F32),
            dma((hh, n_dev - 1)), dma((hh, n_dev)), dma((2, hh)), dma((2, hh)), dma((2,)), dma((2,)),
            dma((hh, n_dev - 1)), dma((heads, n_chip)), dma((2, 2)), dma((2, 2))],
        compiler_params=pltpu.CompilerParams(vmem_limit_bytes=VLIM, collective_id=pair, has_side_effects=True),
        cost_estimate=pl.CostEstimate(flops=flops, bytes_accessed=4 * keys * half, transcendentals=0),
        name=f"global_{pair}")


def solution(mesh):
    n_dev = mesh.shape['ctx']
    n_chip = n_dev // 2
    shift = [(i, i + 1) for i in range(n_dev - 1)]
    row_spec = P(('dp', 'ctx'), None)
    cache_spec = P(None, ('dp', 'ctx'), None, None)
    local_spec = P(None, 'dp', None, None)
    in_specs = (row_spec, P('dp'), cache_spec, cache_spec, local_spec, local_spec) + (P(),) * 9

    def step(x, cache_len, k_cache, v_cache, k_local, v_local, g_attn, g_mlp, w_q, w_k, w_v, w_o, w_gate, w_up, w_down):
        dev_a = lax.axis_index('ctx').astype(jnp.int32).reshape(1)
        rows, d = x.shape
        ff = w_gate.shape[2]
        pairs, slots, _, _ = k_cache.shape
        kc = jnp.transpose(k_cache, (0, 2, 1, 3))
        vc = jnp.transpose(v_cache, (0, 2, 1, 3))
        kl = jnp.transpose(k_local, (0, 2, 1, 3))
        vl = jnp.transpose(v_local, (0, 2, 1, 3))
        q, k, v = layer_kernel(None, 0, rows, d, ff)(x, g_attn, w_q, w_k, w_v)
        for p in range(pairs):
            l = 2 * p
            kh = lax.ppermute(k, 'ctx', shift)
            vh = lax.ppermute(v, 'ctx', shift)
            o = local_attention(p, rows, d, n_chip)(dev_a, q, k, v, kh, vh, kl, vl)
            x, q, k, v = layer_kernel(l, l + 1, rows, d, ff)(
                o, x, g_mlp, g_attn, w_o, w_gate, w_up, w_down, w_q, w_k, w_v)
            o, _, _ = global_attention(p, slots, rows, d, n_chip)(cache_len, q, k, v, kc, vc)
            if p + 1 < pairs:
                x, q, k, v = layer_kernel(l + 1, l + 2, rows, d, ff)(
                    o, x, g_mlp, g_attn, w_o, w_gate, w_up, w_down, w_q, w_k, w_v)
            else:
                x, = layer_kernel(l + 1, None, rows, d, ff)(o, x, g_mlp, w_o, w_gate, w_up, w_down)
        return x

    return jax.shard_map(step, mesh=mesh, in_specs=in_specs, out_specs=row_spec, check_vma=False)
```

profile of v0, /device:TPU:0, one launch (start us, length us, event | category | flops | bytes accessed | tf_op | source)
XLA Modules:
  0.0 776.2 jit_solution(18362369553919708224)
XLA Ops:
  0.0 18.0 %layer_None_0.1 = (bf16[256,2560]{1,0:T(8,128)(2,1)}, bf16[256,2560]{1,0:T(8,128)(2,1)}, bf16[256,2560]{1,0:T(8,128)(2,1)}) custom-call(bf16[256,2560]{1,0:T(8,128)(2,1)} %refs_1_.3, bf16[4,2560]{1,0:T(4,128)(2,1)} %refs_3_.8, bf16[4,2560,2560]{2,1,0:T(8,128)(2,1)} %refs_8_.5, bf16[4,2560,2560]{2,1,0:T(8,128)(2,1)} %refs_9_.5, bf16[4,2560,2560]{2,1,0:T(8,128)(2,1)} %refs_10_.5), custom_call_target="tpu_custom_call" | custom-call | flops 10066329600 | bytes 39321600 | tf_op jit(solution)/shard_map/layer_None_0/pallas_call | solution.py:430
  18.1 2.8 collective-permute-start
  20.9 4.5 collective-permute-start.1
  26.1 0.0 collective-permute-done.kh_ref
  26.1 0.0 copy-start
  26.1 1.9 collective-permute-done.1.vh_ref
  28.0 0.0 copy-start.1
  28.0 0.0 copy-done
  28.0 1.1 copy-done.1
  29.1 13.5 %local_0.1.refs_0_ = bf16[256,2560]{1,0:T(8,128)(2,1)} custom-call(s32[1]{0:T(128)} %bitcast.dev_ref, bf16[256,2560]{1,0:T(8,128)(2,1)} %get-tuple-element.22.q_ref, bf16[256,2560]{1,0:T(8,128)(2,1)} %get-tuple-element.23.k_ref, bf16[256,2560]{1,0:T(8,128)(2,1)} %get-tuple-element.24.v_ref, bf16[256,2560]{1,0:T(8,128)(2,1)} %copy-done, ...), custom_call_target="tpu_custom_call" | custom-call | flops 1342177280 | bytes 10485760 | tf_op jit(solution)/shard_map/local_0/pallas_call | solution.py:435
  42.6 76.3 %layer_0_1.1 = (bf16[256,2560]{1,0:T(8,128)(2,1)}, bf16[256,2560]{1,0:T(8,128)(2,1)}, bf16[256,2560]{1,0:T(8,128)(2,1)}, bf16[256,2560]{1,0:T(8,128)(2,1)}) custom-call(bf16[256,2560]{1,0:T(8,128)(2,1)} %local_0.1.refs_0_, bf16[256,2560]{1,0:T(8,128)(2,1)} %refs_1_.3, bf16[4,2560]{1,0:T(4,128)(2,1)} %refs_2_.9, bf16[4,2560]{1,0:T(4,128)(2,1)} %refs_3_.8, ...), custom_call_target="tpu_custom_call" | custom-call | flops 53687091200 | bytes 209715200 | tf_op jit(solution)/shard_map/layer_0_1/pallas_call | solution.py:436
  118.9 210.1 %global_0.1 = (bf16[256,2560]{1,0:T(8,128)(2,1)}, bf16[10,2048,128]{2,1,0:T(8,128)(2,1)}, bf16[10,2048,128]{2,1,0:T(8,128)(2,1)}) custom-call(s32[1]{0:T(128)S(6)} %copy.16.len_ref, bf16[256,2560]{1,0:T(8,128)(2,1)} %get-tuple-element.25.q_ref, bf16[256,2560]{1,0:T(8,128)(2,1)} %get-tuple-element.26.kn_ref, bf16[256,2560]{1,0:T(8,128)(2,1)} %get-tuple-element.27.vn_ref, ...), custom_call_target="tpu_custom_call" | custom-call | flops 48318382080 | bytes 23592960 | tf_op jit(solution)/shard_map/global_0/pallas_call | solution.py:438
  329.1 76.5 %layer_1_2.1 = (bf16[256,2560]{1,0:T(8,128)(2,1)}, bf16[256,2560]{1,0:T(8,128)(2,1)}, bf16[256,2560]{1,0:T(8,128)(2,1)}, bf16[256,2560]{1,0:T(8,128)(2,1)}) custom-call(bf16[256,2560]{1,0:T(8,128)(2,1)} %get-tuple-element.28.refs_0_, bf16[256,2560]{1,0:T(8,128)(2,1)} %get-tuple-element.29.refs_1_, bf16[4,2560]{1,0:T(4,128)(2,1)} %refs_2_.9, ...), custom_call_target="tpu_custom_call" | custom-call | flops 53687091200 | bytes 209715200 | tf_op jit(solution)/shard_map/layer_1_2/pallas_call | solution.py:440
  405.6 4.0 collective-permute-start.2
  409.6 1.9 collective-permute-start.3
  411.5 0.6 collective-permute-done.2.kh_ref
  412.2 0.0 copy-start.2
  412.2 1.9 collective-permute-done.3.vh_ref
  414.1 0.0 copy-start.3
  414.1 0.0 copy-done.2
  414.1 1.1 copy-done.3
  415.2 13.5 %local_1.1.refs_0_ = bf16[256,2560]{1,0:T(8,128)(2,1)} custom-call(s32[1]{0:T(128)} %bitcast.dev_ref, bf16[256,2560]{1,0:T(8,128)(2,1)} %get-tuple-element.30.q_ref, bf16[256,2560]{1,0:T(8,128)(2,1)} %get-tuple-element.31.k_ref, bf16[256,2560]{1,0:T(8,128)(2,1)} %get-tuple-element.32.v_ref, bf16[256,2560]{1,0:T(8,128)(2,1)} %copy-done.2, ...), custom_call_target="tpu_custom_call" | custom-call | flops 1342177280 | bytes 10485760 | tf_op jit(solution)/shard_map/local_1/pallas_call | solution.py:435
  428.7 76.3 %layer_2_3.1 = (bf16[256,2560]{1,0:T(8,128)(2,1)}, bf16[256,2560]{1,0:T(8,128)(2,1)}, bf16[256,2560]{1,0:T(8,128)(2,1)}, bf16[256,2560]{1,0:T(8,128)(2,1)}) custom-call(bf16[256,2560]{1,0:T(8,128)(2,1)} %local_1.1.refs_0_, bf16[256,2560]{1,0:T(8,128)(2,1)} %get-tuple-element.33.refs_1_, bf16[4,2560]{1,0:T(4,128)(2,1)} %refs_2_.9, bf16[4,2560]{1,0:T(4,128)(2,1)} %refs_3_.8, ...), custom_call_target="tpu_custom_call" | custom-call | flops 53687091200 | bytes 209715200 | tf_op jit(solution)/shard_map/layer_2_3/pallas_call | solution.py:436
  505.0 209.4 %global_1.1 = (bf16[256,2560]{1,0:T(8,128)(2,1)}, bf16[10,2048,128]{2,1,0:T(8,128)(2,1)}, bf16[10,2048,128]{2,1,0:T(8,128)(2,1)}) custom-call(s32[1]{0:T(128)S(6)} %copy.16.len_ref, bf16[256,2560]{1,0:T(8,128)(2,1)} %get-tuple-element.34.q_ref, bf16[256,2560]{1,0:T(8,128)(2,1)} %get-tuple-element.35.kn_ref, bf16[256,2560]{1,0:T(8,128)(2,1)} %get-tuple-element.36.vn_ref, ...), custom_call_target="tpu_custom_call" | custom-call | flops 48318382080 | bytes 23592960 | tf_op jit(solution)/shard_map/global_1/pallas_call | solution.py:438
  714.4 61.4 %layer_3_None.1 = bf16[256,2560]{1,0:T(8,128)(2,1)} custom-call(bf16[256,2560]{1,0:T(8,128)(2,1)} %get-tuple-element.37.refs_0_, bf16[256,2560]{1,0:T(8,128)(2,1)} %get-tuple-element.38.refs_1_, bf16[4,2560]{1,0:T(4,128)(2,1)} %refs_2_.9, bf16[4,2560,2560]{2,1,0:T(8,128)(2,1)} %refs_3_.9, bf16[4,2560,10240]{2,1,0:T(8,128)(2,1)} %refs_4_.9, ...), custom_call_target="tpu_custom_call" | custom-call | flops 43620761600 | bytes 170393600 | tf_op jit(solution)/shard_map/layer_3_None/pallas_call | solution.py:443
Async XLA Ops:
  18.1 8.0 %collective-permute-start = (bf16[256,2560]{1,0:T(8,128)(2,1)}, bf16[256,2560]{1,0:T(8,128)(2,1)S(1)}, u32[]{:S(2)}, u32[]{:S(2)}) collective-permute-start(bf16[256,2560]{1,0:T(8,128)(2,1)} %get-tuple-element.23.k_ref), channel_id=1, source_target_pairs={{0,1},{1,2},{2,3},{3,4},{4,5},{5,6},{6,7}} | collective-permute-start | bytes 3932168 | tf_op jit(solution)/shard_map/ppermute | solution.py:433
  20.9 7.1 collective-permute-start.1
  26.1 1.9 copy-start
  28.0 1.1 copy-start.1
  405.6 6.6 collective-permute-start.2
  409.6 4.5 collective-permute-start.3
  412.2 1.9 copy-start.2
  414.1 1.1 copy-start.3
where the time goes:
time: 784 us; the launch traced here: 776 us
  Pallas kernels  755 us (96%)
  starting transfers between devices  13.3 us (2%)
    pallas_call x2, Pallas kernels, step(): global_attention(p, slots, rows, d, n_chip)(cache_len, q, k, v, kc, vc)  420 us
    pallas_call x2, Pallas kernels, step(): layer_kernel(l, l + 1, rows, d, ff)  153 us
    pallas_call x1, Pallas kernels, step(): layer_kernel(l + 1, l + 2, rows, d, ff)  76.5 us
    pallas_call x1, Pallas kernels, step(): layer_kernel(l + 1, None, rows, d, ff)  61.4 us
    pallas_call x2, Pallas kernels, step(): o = local_attention(p, rows, d, n_chip)(dev_a, q, k, v, kh, vh, kl, vl)  27 us
    pallas_call x1, Pallas kernels, step(): q, k, v = layer_kernel(None, 0, rows, d, ff)(x, g_attn, w_q, w_k, w_v)  18 us
  transfers between devices with their start and end apart: 4, of which 3 were waited for; matrix products, arithmetic and copies ran while one was open for 0% of the time, Pallas kernels for 0%

commit v1 on v0

v1 whole, which is shorter than its diff:
```python
import functools
import jax
import jax.numpy as jnp
from jax import lax
from jax.experimental import pallas as pl
from jax.experimental.pallas import tpu as pltpu
from jax.sharding import PartitionSpec as P

EPS = 1e-6
CH = 512
NS = 3
KT = 1024
HU = 5
HD = 128
LOG2E = 1.4426950408889634
SCALE2 = LOG2E * HD ** -0.5
NEG = -jnp.inf
BF = jnp.bfloat16
F32 = jnp.float32
VLIM = 60 * 2 ** 20

VM = pl.BlockSpec(memory_space=pltpu.VMEM)
HB = pl.BlockSpec(memory_space=pl.ANY)
SM = pl.BlockSpec(memory_space=pltpu.SMEM)


def norm_rows(xf, gain):
    inv = lax.rsqrt(jnp.mean(xf * xf, axis=-1, keepdims=True) + EPS)
    return (xf * inv * gain).astype(BF)


def col(c, w):
    return pl.ds(pl.multiple_of(c * w, w), w)


def layer_kernel(layer, nxt, rows, d, ff, local=None, n_proj=3):
    has_tail = layer is not None
    early = local is not None
    heads = d // HD
    na = d // CH if has_tail else 0
    nb = ff // CH if has_tail else 0
    nc = d // CH if nxt is not None else 0
    total = na + nb + nc

    def body(*refs):
        refs = list(refs)

        def take(n):
            out = refs[:n]
            del refs[:n]
            return out
        if local is not None:
            dev_ref, qi_ref, ki_ref, vi_ref, kh_ref, vh_ref, kl_ref, vl_ref = take(8)
        elif has_tail:
            o_ref, = take(1)
        x_ref, = take(1)
        if has_tail:
            gm_ref, = take(1)
        if nc:
            ga_ref, = take(1)
        if has_tail:
            wo, wg, wu, wd = take(4)
        if nc:
            qkv_w = take(n_proj)
        if has_tail:
            xo_ref, = take(1)
        if nc:
            qkv_refs = take(n_proj)
        ba, bb, bc, bd, h_s, acc, sa, sb, sc, sd = take(10)
        if local is not None:
            o_ref, kl_s, vl_s, sl = take(4)

        def cp(w, l, c, buf, sem, slot, by_rows=False):
            src = w.at[l, pl.ds(pl.multiple_of(c * CH, CH), CH), :] if by_rows else w.at[l, :, col(c, CH)]
            return pltpu.make_async_copy(src, buf.at[slot], sem.at[slot])

        def start(t):
            slot = lax.rem(t, NS)
            if has_tail:
                @pl.when(t < na)
                def _():
                    cp(wo, layer, t, bd, sd, slot, True).start()

                @pl.when((t >= na + (NS if early else 0)) & (t < na + nb))
                def _():
                    cp(wg, layer, t - na, ba, sa, slot).start()
                    cp(wu, layer, t - na, bb, sb, slot).start()

                @pl.when((t >= na) & (t < na + nb))
                def _():
                    cp(wd, layer, t - na, bd, sd, slot, True).start()
            if nc:
                @pl.when((t >= na + nb) & (t < total))
                def _():
                    for w, buf, sem in zip(qkv_w, (ba, bb, bc), (sa, sb, sc)):
                        cp(w, nxt, t - na - nb, buf, sem, slot).start()

        def ahead(t):
            if early:
                @pl.when(t >= 1)
                def _():
                    start(t + NS - 1)
            else:
                start(t + NS - 1)

        if local is not None:
            fetch = [pltpu.make_async_copy(src.at[local], dst, sl.at[i])
                     for i, (src, dst) in enumerate(((kl_ref, kl_s), (vl_ref, vl_s)))]
            for f in fetch:
                f.start()
        for t in range(NS if early else NS - 1):
            start(jnp.int32(t))
        if has_tail:
            for c in range(NS if early else 0):
                cp(wg, layer, c, ba, sa, (na + c) % NS).start()
                cp(wu, layer, c, bb, sb, (na + c) % NS).start()
            acc[...] = x_ref[...].astype(F32)
            if local is not None:
                for f in fetch:
                    f.wait()
                first = dev_ref[0] == 0
                key_id = lax.broadcasted_iota(jnp.int32, (rows, rows), 0)
                row_id = lax.broadcasted_iota(jnp.int32, (rows, rows), 1)

                def some_heads(g, _):
                    for j in range(HU):
                        h = g * HU + j
                        c = col(h, HD)
                        q = qi_ref[:, c]
                        kh = jnp.where(first, kl_s[h], kh_ref[:, c])
                        vh = jnp.where(first, vl_s[h], vh_ref[:, c])
                        dims = (((1,), (1,)), ((), ()))
                        sh = lax.dot_general(kh, q, dims, preferred_element_type=F32)
                        so = lax.dot_general(ki_ref[:, c], q, dims, preferred_element_type=F32)
                        sh = jnp.where(key_id > row_id, sh, NEG)
                        so = jnp.where(key_id <= row_id, so, NEG)
                        m = jnp.maximum(jnp.max(sh, axis=0, keepdims=True), jnp.max(so, axis=0, keepdims=True)) * SCALE2
                        ph = jnp.exp2(sh * SCALE2 - m)
                        po = jnp.exp2(so * SCALE2 - m)
                        den = jnp.sum(ph, axis=0, keepdims=True) + jnp.sum(po, axis=0, keepdims=True)
                        dims = (((0,), (0,)), ((), ()))
                        num = (lax.dot_general(vh, ph.astype(BF), dims, preferred_element_type=F32)
                               + lax.dot_general(vi_ref[:, c], po.astype(BF), dims, preferred_element_type=F32))
                        o_ref[:, c] = (num / den).T.astype(BF)
                    return 0
                lax.fori_loop(0, heads // HU, some_heads, 0)

            def pa(t, _):
                ahead(t)
                slot = lax.rem(t, NS)
                cp(wo, layer, 0, bd, sd, slot, True).wait()
                acc[...] += jnp.dot(o_ref[:, col(t, CH)], bd[slot], preferred_element_type=F32)
                return 0
            lax.fori_loop(0, na, pa, 0)
            xm = acc[...].astype(BF).astype(F32)
            h_s[...] = norm_rows(xm, gm_ref[layer:layer + 1, :].astype(F32))
            acc[...] = xm

            def pb(t, _):
                ahead(t)
                slot = lax.rem(t, NS)
                cp(wg, layer, 0, ba, sa, slot).wait()
                gate = jnp.dot(h_s[...], ba[slot], preferred_element_type=F32)
                cp(wu, layer, 0, bb, sb, slot).wait()
                up = jnp.dot(h_s[...], bb[slot], preferred_element_type=F32)
                act = (jax.nn.gelu(gate, approximate=True) * up).astype(BF)
                cp(wd, layer, 0, bd, sd, slot, True).wait()
                acc[...] += jnp.dot(act, bd[slot], preferred_element_type=F32)
                return 0
            lax.fori_loop(na, na + nb, pb, 0)
            xb = acc[...].astype(BF)
            xo_ref[...] = xb
        else:
            xb = x_ref[...]
        if nc:
            h_s[...] = norm_rows(xb.astype(F32), ga_ref[nxt:nxt + 1, :].astype(F32))

            def pc(t, _):
                ahead(t)
                slot = lax.rem(t, NS)
                for w, buf, sem, r in zip(qkv_w, (ba, bb, bc), (sa, sb, sc), qkv_refs):
                    cp(w, nxt, 0, buf, sem, slot).wait()
                    r[:, col(t - na - nb, CH)] = jnp.dot(h_s[...], buf[slot], preferred_element_type=F32).astype(BF)
                return 0
            lax.fori_loop(na + nb, total, pc, 0)

    specs = []
    if local is not None:
        specs += [SM] + [VM] * 5 + [HB] * 2
    elif has_tail:
        specs += [VM]
    specs += [VM] * (1 + (1 if has_tail else 0) + (1 if nc else 0))
    specs += [HB] * ((4 if has_tail else 0) + (n_proj if nc else 0))
    n_out = (1 if has_tail else 0) + (n_proj if nc else 0)
    flops = 2 * rows * d * ((d + 3 * ff if has_tail else 0) + (n_proj * d if nc else 0))
    dma = pltpu.SemaphoreType.DMA
    scratch = [
        pltpu.VMEM((NS, d, CH), BF), pltpu.VMEM((NS, d, CH), BF),
        pltpu.VMEM((NS, d, CH) if nc else (NS, 16, CH), BF), pltpu.VMEM((NS, CH, d), BF),
        pltpu.VMEM((rows, d), BF), pltpu.VMEM((rows, d), F32), dma((NS,)), dma((NS,)), dma((NS,)), dma((NS,))]
    if local is not None:
        scratch += [pltpu.VMEM((rows, d), BF), pltpu.VMEM((heads, rows, HD), BF), pltpu.VMEM((heads, rows, HD), BF), dma((2,))]
    return pl.pallas_call(
        body, out_shape=[jax.ShapeDtypeStruct((rows, d), BF)] * n_out, in_specs=specs, out_specs=[VM] * n_out,
        scratch_shapes=scratch,
        compiler_params=pltpu.CompilerParams(vmem_limit_bytes=VLIM),
        cost_estimate=pl.CostEstimate(flops=flops, bytes_accessed=flops // rows, transcendentals=0),
        name=f"layer_{layer}_{nxt}_{n_proj}")


def global_attention(pair, slot_rows, rows, d, n_chip):
    n_dev = 2 * n_chip
    nq = n_dev * rows
    qh = nq // 2
    heads = d // HD
    hh = heads // 2
    half = hh * HD
    cache = 2 * slot_rows
    keys = cache + 2 * rows
    st = HD + 8
    n_tile = cache // KT
    low = -3e38

    def body(len_ref, q_ref, kn_ref, vn_ref, kc, vc, o_ref, kx, vx,
             qb, knp, vnp, ks, vs, cap, m_s, l_s, acc, s_a, s_b, stage, part,
             q_snd, q_rcv, x_snd, x_rcv, n_snd, n_rcv, p_snd, p_rcv, sk, sv):
        dev = lax.axis_index('ctx')
        core = lax.rem(dev, 2)
        g_me = lax.div(dev, 2)
        mate = dev + 1 - 2 * core

        def remote(src, dst, snd, rcv, to):
            return pltpu.make_async_remote_copy(
                src_ref=src, dst_ref=dst, send_sem=snd, recv_sem=rcv,
                device_id={'ctx': to}, device_id_type=pl.DeviceIdType.MESH)

        def head_cols(b, i):
            return pl.ds(pl.multiple_of((b * hh + i) * HD, HD), HD)

        def dev_rows(t):
            return pl.ds(pl.multiple_of(t * rows, rows), rows)

        def q_copy(i, k):
            to = lax.rem(dev + k, n_dev)
            return remote(q_ref.at[:, head_cols(lax.rem(to, 2), i)], qb.at[i, dev_rows(dev), :],
                          q_snd.at[i, k - 1], q_rcv.at[i, dev], to)

        def q_wait(i, k):
            src = lax.rem(dev + k, n_dev)
            remote(q_ref.at[:, head_cols(0, i)], qb.at[i, dev_rows(src), :],
                   q_snd.at[i, k - 1], q_rcv.at[i, src], src).wait_recv()

        def x_copy(i, w):
            src, dst = ((kc, kx), (vc, vx))[w]
            return remote(src.at[pair, (1 - core) * hh + i], dst.at[i], x_snd.at[w, i], x_rcv.at[w, i], mate)

        def n_copy(w):
            src, dst = ((kn_ref, knp), (vn_ref, vnp))[w]
            return remote(src.at[:, pl.ds(pl.multiple_of((1 - core) * half, half), half)], dst,
                          n_snd.at[w], n_rcv.at[w], mate)

        def p_copy(i, to):
            return remote(stage.at[i, to], part.at[core * hh + i, g_me],
                          p_snd.at[i, to], p_rcv.at[core * hh + i, g_me], to)

        def own(i, slot, w):
            src, dst, sem = ((kc, ks, sk), (vc, vs, sv))[w]
            return pltpu.make_async_copy(src.at[pair, core * hh + i], dst.at[slot, 0:slot_rows, :], sem.at[slot, 0])

        def mated(i, slot, w):
            src, dst, sem = ((kx, ks, sk), (vx, vs, sv))[w]
            return pltpu.make_async_copy(src.at[i], dst.at[slot, slot_rows:cache, :], sem.at[slot, 1])

        bar = pltpu.get_barrier_semaphore()
        for k in range(1, n_dev):
            pl.semaphore_signal(bar, inc=1, device_id={'ctx': lax.rem(dev + k, n_dev)}, device_id_type=pl.DeviceIdType.MESH)
        pl.semaphore_wait(bar, n_dev - 1)

        for w in range(2):
            own(0, 0, w).start()
            x_copy(0, w).start()
            n_copy(w).start()

        def send_q(i, _):
            for k in range(1, n_dev):
                q_copy(i, k).start()
            return 0
        lax.fori_loop(0, hh, send_q, 0)

        def send_x(i, _):
            for w in range(2):
                x_copy(i, w).start()
            return 0
        lax.fori_loop(1, hh, send_x, 0)
        for w in range(2):
            x_copy(0, w).wait_recv()
            mated(0, 0, w).start()
            n_copy(w).wait_recv()

        n = len_ref[0]
        for t, owner in enumerate((dev, mate)):
            left = n - owner * slot_rows
            cap[t * slot_rows:(t + 1) * slot_rows, :] = jnp.where(
                lax.broadcasted_iota(jnp.int32, (slot_rows, HD), 0) < left, -NEG, NEG)

        def one_head(i, _):
            slot = lax.rem(i, 2)

            @pl.when(i + 1 < hh)
            def _():
                for w in range(2):
                    own(i + 1, 1 - slot, w).start()
                    x_copy(i + 1, w).wait_recv()
                    mated(i + 1, 1 - slot, w).start()
            mine = head_cols(core, i)
            there = head_cols(0, i)
            ks[slot, cache:cache + rows, :] = kn_ref[:, mine]
            ks[slot, cache + rows:keys, :] = knp[:, there]
            vs[slot, cache:cache + rows, :] = vn_ref[:, mine]
            vs[slot, cache + rows:keys, :] = vnp[:, there]
            qb[i, dev_rows(dev), :] = q_ref[:, mine]
            for k in range(1, n_dev):
                q_wait(i, k)
            for w in range(2):
                own(i, slot, w).wait()
                mated(i, slot, w).wait()

            def one_half(hf, _):
                q = qb[i, pl.ds(pl.multiple_of(hf * qh, qh), qh), :]
                m_s[...] = jnp.full(m_s.shape, low, F32)
                l_s[...] = jnp.zeros(l_s.shape, F32)
                acc[...] = jnp.zeros(acc.shape, F32)

                def scores(start, size):
                    k = ks[slot, start:start + size, :]
                    return lax.dot_general(k, q, (((1,), (1,)), ((), ())), preferred_element_type=F32)

                def absorb(s, start, size):
                    v = vs[slot, start:start + size, :]
                    m0 = m_s[...]
                    m1 = jnp.maximum(m0, jnp.max(s, axis=0, keepdims=True))
                    a = jnp.exp2((m0 - m1) * SCALE2)
                    p = jnp.exp2(s * SCALE2 - m1 * SCALE2)
                    l_s[...] = l_s[...] * a + jnp.sum(p, axis=0, keepdims=True)
                    m_s[...] = m1
                    acc[...] = acc[...] * a + lax.dot_general(v, p.astype(BF), (((0,), (0,)), ((), ())), preferred_element_type=F32)

                def valid(s, t):
                    lim = cap[t * KT:(t + 1) * KT, :]
                    return jnp.minimum(s, jnp.concatenate([lim] * (qh // HD), axis=1))

                bufs = (s_a, s_b)
                s_b[0:2 * rows, :] = scores(cache, 2 * rows)
                s_a[...] = scores(0, KT)
                s = s_b[0:2 * rows, :]
                r = lax.broadcasted_iota(jnp.int32, s.shape, 0)
                qi = lax.broadcasted_iota(jnp.int32, s.shape, 1) + hf * qh
                pos = jnp.where(r < rows, r + dev * rows, r - rows + mate * rows)
                absorb(jnp.where(pos <= qi, s, NEG), cache, 2 * rows)
                for t in range(n_tile):
                    if t + 1 < n_tile:
                        bufs[(t + 1) % 2][...] = scores((t + 1) * KT, KT)
                    absorb(valid(bufs[t % 2][...], t), t * KT, KT)
                for t in range(n_chip):
                    c = slice(t * rows, (t + 1) * rows)
                    to = hf * n_chip + t
                    stage[i, to, 0:HD, :] = acc[:, c]
                    stage[i, to, HD:HD + 1, :] = m_s[:, c]
                    stage[i, to, HD + 1:HD + 2, :] = l_s[:, c]
                for t in range(n_chip):
                    to = hf * n_chip + t

                    @pl.when(to != dev)
                    def _():
                        p_copy(i, to).start()

                    @pl.when(to == dev)
                    def _():
                        part[core * hh + i, g_me] = stage[i, to]
                return 0
            lax.fori_loop(0, 2, one_half, 0)
            return 0
        lax.fori_loop(0, hh, one_head, 0)

        def finish(i, _):
            for b in range(2):
                h = b * hh + i
                for g in range(n_chip):
                    src = 2 * g + b

                    @pl.when(src != dev)
                    def _():
                        remote(stage.at[i, 0], part.at[h, g], p_snd.at[i, 0], p_rcv.at[h, g], mate).wait_recv()
                m = [part[h, g, HD:HD + 1, :] for g in range(n_chip)]
                top = functools.reduce(jnp.maximum, m)
                num = 0.0
                den = 0.0
                for g in range(n_chip):
                    a = jnp.exp2((m[g] - top) * SCALE2)
                    num = num + part[h, g, 0:HD, :] * a
                    den = den + part[h, g, HD + 1:HD + 2, :] * a
                o_ref[:, head_cols(b, i)] = (num / den).T.astype(BF)
            return 0
        lax.fori_loop(0, hh, finish, 0)

        def drain(i, _):
            for k in range(1, n_dev):
                q_copy(i, k).wait_send()
                p_copy(i, lax.rem(dev + k, n_dev)).wait_send()
            for w in range(2):
                x_copy(i, w).wait_send()
            return 0
        lax.fori_loop(0, hh, drain, 0)
        for w in range(2):
            n_copy(w).wait_send()

    flops = 4 * nq * keys * half
    dma = pltpu.SemaphoreType.DMA
    xs = jax.ShapeDtypeStruct((hh, slot_rows, HD), BF)
    return pl.pallas_call(
        body, out_shape=[jax.ShapeDtypeStruct((rows, d), BF), xs, xs],
        in_specs=[SM, VM, VM, VM, HB, HB], out_specs=[VM, HB, HB],
        scratch_shapes=[
            pltpu.VMEM((hh, nq, HD), BF), pltpu.VMEM((rows, half), BF), pltpu.VMEM((rows, half), BF),
            pltpu.VMEM((2, keys, HD), BF), pltpu.VMEM((2, keys, HD), BF),
            pltpu.VMEM((cache, HD), F32), pltpu.VMEM((1, qh), F32), pltpu.VMEM((1, qh), F32), pltpu.VMEM((HD, qh), F32),
            pltpu.VMEM((KT, qh), F32), pltpu.VMEM((KT, qh), F32),
            pltpu.VMEM((hh, n_dev, st, rows), F32), pltpu.VMEM((heads, n_chip, st, rows), F32),
            dma((hh, n_dev - 1)), dma((hh, n_dev)), dma((2, hh)), dma((2, hh)), dma((2,)), dma((2,)),
            dma((hh, n_dev)), dma((heads, n_chip)), dma((2, 2)), dma((2, 2))],
        compiler_params=pltpu.CompilerParams(vmem_limit_bytes=VLIM, collective_id=pair, has_side_effects=True),
        cost_estimate=pl.CostEstimate(flops=flops, bytes_accessed=4 * keys * half, transcendentals=0),
        name=f"global_{pair}")


def solution(mesh):
    n_dev = mesh.shape['ctx']
    n_chip = n_dev // 2
    shift = [(i, i + 1) for i in range(n_dev - 1)]
    row_spec = P(('dp', 'ctx'), None)
    cache_spec = P(None, ('dp', 'ctx'), None, None)
    local_spec = P(None, 'dp', None, None)
    in_specs = (row_spec, P('dp'), cache_spec, cache_spec, local_spec, local_spec) + (P(),) * 9

    def step(x, cache_len, k_cache, v_cache, k_local, v_local, g_attn, g_mlp, w_q, w_k, w_v, w_o, w_gate, w_up, w_down):
        dev_a = lax.axis_index('ctx').astype(jnp.int32).reshape(1)
        rows, d = x.shape
        ff = w_gate.shape[2]
        pairs, slots, _, _ = k_cache.shape
        kc = jnp.transpose(k_cache, (0, 2, 1, 3))
        vc = jnp.transpose(v_cache, (0, 2, 1, 3))
        kl = jnp.transpose(k_local, (0, 2, 1, 3))
        vl = jnp.transpose(v_local, (0, 2, 1, 3))
        for p in range(pairs):
            l = 2 * p
            xh = lax.ppermute(x, 'ctx', shift)
            q, k, v = layer_kernel(None, l, rows, d, ff)(x, g_attn, w_q, w_k, w_v)
            kh, vh = layer_kernel(None, l, rows, d, ff, n_proj=2)(xh, g_attn, w_k, w_v)
            x, q, k, v = layer_kernel(l, l + 1, rows, d, ff, local=p)(
                dev_a, q, k, v, kh, vh, kl, vl, x, g_mlp, g_attn, w_o, w_gate, w_up, w_down, w_q, w_k, w_v)
            o, _, _ = global_attention(p, slots, rows, d, n_chip)(cache_len, q, k, v, kc, vc)
            x, = layer_kernel(l + 1, None, rows, d, ff)(o, x, g_mlp, w_o, w_gate, w_up, w_down)
        return x

    return jax.shard_map(step, mesh=mesh, in_specs=in_specs, out_specs=row_spec, check_vma=False)
```

time: 784 us -> 750 us (0.957)
  Pallas kernels: 755 us -> 732 us
    pallas_call x1 -> x2, Pallas kernels: 61.4 us -> 123 us  [step(): layer_kernel(l + 1, None, rows, d, ff)]
    pallas_call x2, Pallas kernels: 420 us -> 372 us  [step(): global_attention(p, slots, rows, d, n_chip)(cache_len, q, k, v, kc, vc)]
    pallas_call x6, Pallas kernels: 274 us -> 237 us  [the longest x2 178 us: step(): layer_kernel(l, l + 1, rows, d, ff, local=p)]
  transfers between devices with their start and end apart: 4 -> 2, of which waited for: 3 -> 0; matrix products, arithmetic and copies ran while one was open for 0% -> 0% of each run, Pallas kernels for 0% -> 5%
where the time goes in v1:
time: 750 us; the launch traced here: 742 us
  Pallas kernels  732 us (98%)
    pallas_call x2, Pallas kernels, step(): global_attention(p, slots, rows, d, n_chip)(cache_len, q, k, v, kc, vc)  372 us
    pallas_call x2, Pallas kernels, step(): layer_kernel(l, l + 1, rows, d, ff, local=p)  178 us
    pallas_call x2, Pallas kernels, step(): layer_kernel(l + 1, None, rows, d, ff)  123 us
    pallas_call x2, Pallas kernels, step(): q, k, v = layer_kernel(None, l, rows, d, ff)(x, g_attn, w_q, w_k, w_v)  33.9 us
    pallas_call x2, Pallas kernels, step(): kh, vh = layer_kernel(None, l, rows, d, ff, n_proj=2)(xh, g_attn, w_k, w_v)  25.4 us
  transfers between devices with their start and end apart: 2, of which 0 were waited for; matrix products, arithmetic and copies ran while one was open for 0% of the time, Pallas kernels for 5%

profile of v1, /device:TPU:0, one launch (start us, length us, event | category | flops | bytes accessed | tf_op | source)
XLA Modules:
  0.0 741.7 jit_solution(2764989088953240262)
XLA Ops:
  0.0 2.8 collective-permute-start
  3.5 16.9 %layer_None_0_3.1 = (bf16[256,2560]{1,0:T(8,128)(2,1)}, bf16[256,2560]{1,0:T(8,128)(2,1)}, bf16[256,2560]{1,0:T(8,128)(2,1)}) custom-call(bf16[256,2560]{1,0:T(8,128)(2,1)} %refs_8_.1, bf16[4,2560]{1,0:T(4,128)(2,1)} %refs_10_.3, bf16[4,2560,2560]{2,1,0:T(8,128)(2,1)} %refs_15_.3, bf16[4,2560,2560]{2,1,0:T(8,128)(2,1)} %refs_16_.3, ...), custom_call_target="tpu_custom_call" | custom-call | flops 10066329600 | bytes 39321600 | tf_op jit(solution)/shard_map/layer_None_0_3/pallas_call | solution.py:457
  20.4 0.0 collective-permute-done.refs_0_
  20.4 0.0 copy-start
  20.5 1.1 copy-done
  21.5 12.7 %layer_None_0_2.1 = (bf16[256,2560]{1,0:T(8,128)(2,1)}, bf16[256,2560]{1,0:T(8,128)(2,1)}) custom-call(bf16[256,2560]{1,0:T(8,128)(2,1)} %copy-done, bf16[4,2560]{1,0:T(4,128)(2,1)} %refs_10_.3, bf16[4,2560,2560]{2,1,0:T(8,128)(2,1)} %refs_16_.3, bf16[4,2560,2560]{2,1,0:T(8,128)(2,1)} %refs_17_.3), custom_call_target="tpu_custom_call" | custom-call | flops 6710886400 | bytes 26214400 | tf_op jit(solution)/shard_map/layer_None_0_2/pallas_call | solution.py:458
  34.2 89.1 %layer_0_1_3.1 = (bf16[256,2560]{1,0:T(8,128)(2,1)}, bf16[256,2560]{1,0:T(8,128)(2,1)}, bf16[256,2560]{1,0:T(8,128)(2,1)}, bf16[256,2560]{1,0:T(8,128)(2,1)}) custom-call(s32[1]{0:T(128)} %bitcast.refs_0_, bf16[256,2560]{1,0:T(8,128)(2,1)} %get-tuple-element.25.refs_1_, bf16[256,2560]{1,0:T(8,128)(2,1)} %get-tuple-element.26.refs_2_, ...), custom_call_target="tpu_custom_call" | custom-call | flops 53687091200 | bytes 209715200 | tf_op jit(solution)/shard_map/layer_0_1_3/pallas_call | solution.py:459
  123.3 186.5 %global_0.1 = (bf16[256,2560]{1,0:T(8,128)(2,1)}, bf16[10,2048,128]{2,1,0:T(8,128)(2,1)}, bf16[10,2048,128]{2,1,0:T(8,128)(2,1)}) custom-call(s32[1]{0:T(128)S(6)} %copy.16.len_ref, bf16[256,2560]{1,0:T(8,128)(2,1)} %get-tuple-element.30.q_ref, bf16[256,2560]{1,0:T(8,128)(2,1)} %get-tuple-element.31.kn_ref, bf16[256,2560]{1,0:T(8,128)(2,1)} %get-tuple-element.32.vn_ref, ...), custom_call_target="tpu_custom_call" | custom-call | flops 48318382080 | bytes 23592960 | tf_op jit(solution)/shard_map/global_0/pallas_call | solution.py:461
  309.9 61.4 %layer_1_None_3.1.refs_0_.refs_8_ = bf16[256,2560]{1,0:T(8,128)(2,1)} custom-call(bf16[256,2560]{1,0:T(8,128)(2,1)} %get-tuple-element.33.refs_0_, bf16[256,2560]{1,0:T(8,128)(2,1)} %get-tuple-element.34.refs_1_, bf16[4,2560]{1,0:T(4,128)(2,1)} %refs_2_.11, bf16[4,2560,2560]{2,1,0:T(8,128)(2,1)} %refs_3_.11, bf16[4,2560,10240]{2,1,0:T(8,128)(2,1)} %refs_4_.7, ...), custom_call_target="tpu_custom_call" | custom-call | flops 43620761600 | bytes 170393600 | tf_op jit(solution)/shard_map/layer_1_None_3/pallas_call | solution.py:462
  371.3 3.8 collective-permute-start.1
  375.1 16.9 %layer_None_2_3.1 = (bf16[256,2560]{1,0:T(8,128)(2,1)}, bf16[256,2560]{1,0:T(8,128)(2,1)}, bf16[256,2560]{1,0:T(8,128)(2,1)}) custom-call(bf16[256,2560]{1,0:T(8,128)(2,1)} %layer_1_None_3.1.refs_0_.refs_8_, bf16[4,2560]{1,0:T(4,128)(2,1)} %refs_10_.3, bf16[4,2560,2560]{2,1,0:T(8,128)(2,1)} %refs_15_.3, bf16[4,2560,2560]{2,1,0:T(8,128)(2,1)} %refs_16_.3, ...), custom_call_target="tpu_custom_call" | custom-call | flops 10066329600 | bytes 39321600 | tf_op jit(solution)/shard_map/layer_None_2_3/pallas_call | solution.py:457
  392.0 0.0 collective-permute-done.1.refs_0_
  392.0 0.0 copy-start.1
  392.0 1.0 copy-done.1
  393.1 12.7 %layer_None_2_2.1 = (bf16[256,2560]{1,0:T(8,128)(2,1)}, bf16[256,2560]{1,0:T(8,128)(2,1)}) custom-call(bf16[256,2560]{1,0:T(8,128)(2,1)} %copy-done.1, bf16[4,2560]{1,0:T(4,128)(2,1)} %refs_10_.3, bf16[4,2560,2560]{2,1,0:T(8,128)(2,1)} %refs_16_.3, bf16[4,2560,2560]{2,1,0:T(8,128)(2,1)} %refs_17_.3), custom_call_target="tpu_custom_call" | custom-call | flops 6710886400 | bytes 26214400 | tf_op jit(solution)/shard_map/layer_None_2_2/pallas_call | solution.py:458
  405.8 89.1 %layer_2_3_3.1 = (bf16[256,2560]{1,0:T(8,128)(2,1)}, bf16[256,2560]{1,0:T(8,128)(2,1)}, bf16[256,2560]{1,0:T(8,128)(2,1)}, bf16[256,2560]{1,0:T(8,128)(2,1)}) custom-call(s32[1]{0:T(128)} %bitcast.refs_0_, bf16[256,2560]{1,0:T(8,128)(2,1)} %get-tuple-element.35.refs_1_, bf16[256,2560]{1,0:T(8,128)(2,1)} %get-tuple-element.36.refs_2_, ...), custom_call_target="tpu_custom_call" | custom-call | flops 53687091200 | bytes 209715200 | tf_op jit(solution)/shard_map/layer_2_3_3/pallas_call | solution.py:459
  494.9 185.0 %global_1.1 = (bf16[256,2560]{1,0:T(8,128)(2,1)}, bf16[10,2048,128]{2,1,0:T(8,128)(2,1)}, bf16[10,2048,128]{2,1,0:T(8,128)(2,1)}) custom-call(s32[1]{0:T(128)S(6)} %copy.16.len_ref, bf16[256,2560]{1,0:T(8,128)(2,1)} %get-tuple-element.40.q_ref, bf16[256,2560]{1,0:T(8,128)(2,1)} %get-tuple-element.41.kn_ref, bf16[256,2560]{1,0:T(8,128)(2,1)} %get-tuple-element.42.vn_ref, ...), custom_call_target="tpu_custom_call" | custom-call | flops 48318382080 | bytes 23592960 | tf_op jit(solution)/shard_map/global_1/pallas_call | solution.py:461
  679.9 61.4 %layer_3_None_3.1 = bf16[256,2560]{1,0:T(8,128)(2,1)} custom-call(bf16[256,2560]{1,0:T(8,128)(2,1)} %get-tuple-element.43.refs_0_, bf16[256,2560]{1,0:T(8,128)(2,1)} %get-tuple-element.44.refs_1_, bf16[4,2560]{1,0:T(4,128)(2,1)} %refs_2_.11, bf16[4,2560,2560]{2,1,0:T(8,128)(2,1)} %refs_3_.11, bf16[4,2560,10240]{2,1,0:T(8,128)(2,1)} %refs_4_.7, ...), custom_call_target="tpu_custom_call" | custom-call | flops 43620761600 | bytes 170393600 | tf_op jit(solution)/shard_map/layer_3_None_3/pallas_call | solution.py:462
Async XLA Ops:
  0.0 20.4 %collective-permute-start = (bf16[256,2560]{1,0:T(8,128)(2,1)}, bf16[256,2560]{1,0:T(8,128)(2,1)S(1)}, u32[]{:S(2)}, u32[]{:S(2)}) collective-permute-start(bf16[256,2560]{1,0:T(8,128)(2,1)} %refs_8_.1), channel_id=1, source_target_pairs={{0,1},{1,2},{2,3},{3,4},{4,5},{5,6},{6,7}} | collective-permute-start | bytes 3932168 | tf_op jit(solution)/shard_map/ppermute | solution.py:456
  20.4 1.1 copy-start
  371.3 20.7 %collective-permute-start.1 = (bf16[256,2560]{1,0:T(8,128)(2,1)}, bf16[256,2560]{1,0:T(8,128)(2,1)S(1)}, u32[]{:S(2)}, u32[]{:S(2)}) collective-permute-start(bf16[256,2560]{1,0:T(8,128)(2,1)} %layer_1_None_3.1.refs_0_.refs_8_), channel_id=1, source_target_pairs={{0,1},{1,2},{2,3},{3,4},{4,5},{5,6},{6,7}} | collective-permute-start | bytes 3932168 | tf_op jit(solution)/shard_map/ppermute | solution.py:456
  392.0 1.1 copy-start.1
